TPU v7x, 32 devices: a whole 2x2x4 slice. The times are simulated.
32 devices in a mesh: wide: 8 (over z, y), narrow: 2 (over x), grp: 2 (over core).
Axes of the slice: x: 2, y: 2, z: 4, core: 2. Of those that a mesh axis runs over, the one named last changes fastest.
Arguments:
- boundary_block: float32 [8, 2048, 16384], P(None, ('narrow', 'grp'), 'wide'), may hold values from -4 to 4
- schur_blocks: float32 [2, 1536, 1536], P('narrow', ('wide', 'grp')), may hold values from -2 to 2
- interface_rows: int32 [2, 1536], P('narrow'), may hold values from 0 to 8191, as said below
- live_rows: int32 [2], P('narrow'), may hold values from 1 to 1536, 2304 in all
- row_scale: float32 [8, 2048], P('wide', ('narrow', 'grp')), may hold values from 0.4 to 1.2
- excitation: float32 [8, 2048, 128], P('wide', ('narrow', 'grp')), may hold values from -6 to 6
Outputs:
- traces: float32 [8, 2048, 128], P('wide', ('narrow', 'grp'))
- residual: float32 [8, 2048, 128], P('wide', ('narrow', 'grp'))
Inputs may be any that keep to these rules, and one draw needn't show every extreme that they name: `interface_rows`: each substructure's row holds 1536 different positions, 0 to 8191; within each aligned block of 96 slots, at most 32 positions lie in one aligned range of 512 positions, and every substructure reaches 32 in some block.
All inputs are finite; a program needn't handle non-finite values. No bound on the sum of `live_rows` on one device may be relied on, other than what follows from the above.
Results may differ from a plain program's by a relative error of at most 0.00016.
Values sent between devices are 32-bit elements; how exact they have to be, the bound alone decides.
No kernel may reach another device: no remote copies, remote signals or barrier semaphores. Data moves between devices by JAX's collectives and lax.ppermute only.
A program may use at most 128 MiB of HBM per device.

v0:
```python
import jax
import jax.numpy as jnp
from jax import lax
from jax.sharding import PartitionSpec as P

ITERS = 3
RELAX = 0.35


def slot_ranks(owners):
    count = owners.shape[-1]
    same = owners[..., :, None] == owners[..., None, :]
    earlier = jnp.arange(count)[None, :] < jnp.arange(count)[:, None]
    return jnp.sum((same & earlier).astype(jnp.int32), axis=-1)


def on_device(boundary_block, schur_blocks, interface_rows, live_rows, row_scale, excitation):
    piece_rows = excitation.shape[1]
    wide_size = lax.axis_size("wide")
    grp_size = lax.axis_size("grp")
    blocks = wide_size * grp_size
    panel_size = blocks * piece_rows
    tile_block = boundary_block.reshape(-1, boundary_block.shape[2])
    row_weight = row_scale.reshape(piece_rows, 1)
    forcing = excitation[0]
    iface_size = interface_rows.shape[1]
    share_rows = schur_blocks.shape[1]
    sub_count = interface_rows.shape[0]
    row_group = lax.axis_index("wide") * grp_size + lax.axis_index("grp")
    positions = jnp.arange(iface_size, dtype=jnp.int32)
    live_mask = (positions[None, :] < live_rows[:, None]).astype(jnp.float32)
    own_rows = lax.dynamic_slice_in_dim(interface_rows, row_group * share_rows, share_rows, 1)
    slot_cap = (piece_rows + blocks - 1) // blocks
    targets = jnp.arange(blocks, dtype=jnp.int32)
    levels = jnp.arange(slot_cap, dtype=jnp.int32)
    send_owner = own_rows // piece_rows
    send_rank = slot_ranks(send_owner)
    send_pick = (
        (send_owner[:, None, None, :] == targets[None, :, None, None])
        & (send_rank[:, None, None, :] == levels[None, None, :, None])
    ).astype(jnp.float32)
    outgoing = jnp.einsum(
        "kots,ksm->oktm", send_pick, schur_blocks, precision=lax.Precision.HIGHEST
    )
    received = lax.all_to_all(outgoing, ("wide", "grp"), split_axis=0, concat_axis=0, tiled=True)
    block_rows = interface_rows.reshape(sub_count, blocks, share_rows)
    block_live = live_mask.reshape(sub_count, blocks, share_rows)
    block_owner = block_rows // piece_rows
    block_rank = slot_ranks(block_owner)
    take_pick = (
        (block_owner[:, :, None, :] == row_group)
        & (block_rank[:, :, None, :] == levels[None, None, :, None])
    ).astype(jnp.float32) * block_live[:, :, None, :]
    local_index = jnp.arange(piece_rows, dtype=jnp.int32)
    landing = ((block_rows % piece_rows)[..., None] == local_index).astype(jnp.float32)
    placement = jnp.einsum("kjts,kjsi->kjti", take_pick, landing, precision=lax.Precision.HIGHEST)
    traces = RELAX * row_weight * forcing
    residual = forcing
    for sweep in range(ITERS):
        wide_panel = lax.all_gather(traces[None], "wide", axis=0, tiled=True)
        full_panel = lax.all_gather(wide_panel[:, None], "grp", axis=1, tiled=True)
        stacked = wide_panel.reshape(-1, wide_panel.shape[-1])
        boundary = lax.psum_scatter(
            lax.dot_general(
                tile_block,
                stacked,
                (((0,), (0,)), ((), ())),
                precision=lax.Precision.HIGHEST,
                preferred_element_type=jnp.float32,
            ),
            ("narrow", "grp"),
            scatter_dimension=0,
            tiled=True,
        )
        flat_panel = full_panel.reshape(panel_size, -1)
        local_traces = jnp.take(flat_panel, interface_rows, axis=0) * live_mask[:, :, None]
        values = jnp.einsum(
            "jktm,kmr->kjtr", received, local_traces, precision=lax.Precision.HIGHEST
        )
        interface = jnp.einsum("kjti,kjtr->ir", placement, values, precision=lax.Precision.HIGHEST)
        residual = forcing - (boundary + interface)
        traces = traces + RELAX * row_weight * residual
    return (traces[None], residual[None])


def solution(mesh):
    placed = (
        P(None, ("narrow", "grp"), "wide"),
        P("narrow", ("wide", "grp"), None),
        P("narrow", None),
        P("narrow"),
        P("wide", ("narrow", "grp")),
        P("wide", ("narrow", "grp"), None),
    )
    return jax.shard_map(
        on_device,
        mesh=mesh,
        in_specs=placed,
        out_specs=(P("wide", ("narrow", "grp"), None), P("wide", ("narrow", "grp"), None)),
        check_vma=False,
    )
```

profile of v0, /device:TPU:0, one launch (start us, length us, event | category | flops | bytes accessed | tf_op | source)
XLA Modules:
  0.0 362.8 jit_solution(1860652494400219698)
XLA Ops:
  7.2 0.0 all-gather.12.cloned.1.call-start
  7.2 0.7 broadcast_multiply_fusion.1
  8.0 1.8 broadcast_multiply_fusion
  9.8 0.0 all-gather.14.cloned.1.call-start
  9.8 0.8 fusion.56
  10.6 0.2 convert_reduce_fusion.1
  10.8 51.7 %all-gather.12.cloned.1.call-done = f32[8,512,128]{2,1,0:T(8,128)} async-done(((f32[1,512,128]{2,1,0:T(8,128)}), f32[8,512,128]{2,1,0:T(8,128)}) %all-gather.12.cloned.1.call-update) | async-done | bytes 2097168 | tf_op jit(solution)/shard_map/all_gather | solution.py:60
  62.5 0.0 all-gather.14.cloned.1.call-update
  62.6 3.1 convolution_bitcast_fusion
  65.7 4.7 %all-to-all-start = ((f32[16,1,32,1536]{3,2,1,0:T(8,128)}), f32[16,1,32,1536]{3,2,1,0:T(8,128)}, u32[]{:S(2)}, u32[]{:S(2)}) async-start(f32[16,1,32,1536]{3,2,1,0:T(8,128)} %convolution_bitcast_fusion), calls=%async_computation.1 | async-start | bytes 6291456 | tf_op jit(solution)/shard_map/all_to_all | solution.py:45
  70.4 0.0 reduce-scatter.4.cloned.1.call-start
  70.4 23.7 %convolution_bitcast_fusion.3 = f32[2048,128]{0,1:T(8,128)} fusion(f32[8,512,128]{2,1,0:T(8,128)S(1)} %copy-done.2, f32[8,512,2048]{2,1,0:T(8,128)} %param.8), kind=kOutput, calls=%fused_computation.14 | convolution fusion | flops 12884901888 | bytes 36700160 | tf_op jit(solution)/shard_map/dot_general | solution.py:64
  94.2 0.2 all-gather.16.cloned.1.call-start
  94.4 0.1 copy.43
  95.3 0.1 reshape.475
  95.4 0.6 convert_reduce_fusion
  96.0 1.2 fusion.6
  97.3 0.0 all-gather.14.cloned.1.call-done
  97.3 4.8 %gather_fusion = f32[1536,128]{1,0:T(8,128)S(1)} fusion(f32[8192,128]{1,0:T(8,128)} %bitcast.134, s32[2048]{0:T(1024)S(1)} %pad_clamp_fusion), kind=kCustom, calls=%fused_computation.clone | custom fusion | bytes 1579008 | tf_op jit(solution)/shard_map/jit(_take)/gather | solution.py:76
  102.1 27.5 %all-to-all-done = f32[16,1,32,1536]{3,2,1,0:T(8,128)} async-done(((f32[16,1,32,1536]{3,2,1,0:T(8,128)}), f32[16,1,32,1536]{3,2,1,0:T(8,128)}, u32[]{:S(2)}, u32[]{:S(2)}) %all-to-all-start) | async-done | bytes 3145760 | tf_op jit(solution)/shard_map/all_to_all | solution.py:45
  129.6 4.6 %fusion.4 = f32[16,32,128]{2,1,0:T(8,128)S(1)} fusion(f32[16,1,32,1536]{3,2,1,0:T(8,128)} %all-to-all-done, f32[1536,128]{1,0:T(8,128)S(1)} %gather_fusion, f32[1536]{0:T(1024)S(1)} %fusion.54, pred[1536]{0:T(1024)(128)(4,1)S(1)} %and_reduce_fusion), kind=kOutput, calls=%fused_computation.8 | convolution fusion | flops 1208352768 | bytes 4201984 | tf_op jit(solution)/shard_map/jktm,kmr->kjtr/dot_general | solution.py:77
  134.2 0.0 reduce-scatter.4.cloned.1.call-done
  134.2 2.5 fusion.15
  136.7 0.0 all-gather.18.cloned.1.call-start
  136.8 59.9 %all-gather.16.cloned.1.call-done = f32[4096,128]{0,1:T(8,128)} async-done(((f32[512,128]{0,1:T(8,128)}), f32[4096,128]{0,1:T(8,128)}) %all-gather.16.cloned.1.call-update) | async-done | bytes 2097168 | tf_op jit(solution)/shard_map/all_gather | solution.py:60
  196.6 4.6 %copy.64 = f32[16,8,8,512]{3,2,1,0:T(8,128)} copy(f32[16,8,8,512]{3,1,2,0:T(8,128)} %bitcast.135) | data formatting | bytes 4194304
  201.2 0.3 reduce-scatter.6.cloned.1.call-start
  201.5 23.8 %convolution_bitcast_fusion.2 = f32[2048,128]{0,1:T(8,128)} fusion(f32[8,512,2048]{2,1,0:T(8,128)} %param.8, f32[16,8,8,512]{3,2,1,0:T(8,128)} %bitcast.136), kind=kOutput, calls=%fused_computation.13 | convolution fusion | flops 12884901888 | bytes 36700160 | tf_op jit(solution)/shard_map/dot_general | solution.py:64
  225.3 0.0 all-gather.20.cloned.1.call-start
  225.3 0.0 all-gather.18.cloned.1.call-done
  225.4 5.4 %copy.48 = f32[8,1024,128]{2,1,0:T(8,128)} copy(f32[8,1024,128]{1,0,2:T(8,128)} %all-gather.18.cloned.1.call-done) | data formatting | bytes 8388608 | tf_op jit(solution)/shard_map/all_gather | solution.py:61
  230.7 4.9 %gather_fusion.1 = f32[1536,128]{1,0:T(8,128)S(1)} fusion(f32[8192,128]{1,0:T(8,128)} %bitcast.133, s32[2048]{0:T(1024)S(1)} %pad_clamp_fusion), kind=kCustom, calls=%fused_computation.1.clone | custom fusion | bytes 1579008 | tf_op jit(solution)/shard_map/jit(_take)/gather | solution.py:76
  235.7 4.7 %fusion.2 = f32[16,32,128]{2,1,0:T(8,128)S(1)} fusion(f32[16,1,32,1536]{3,2,1,0:T(8,128)} %all-to-all-done, f32[1536,128]{1,0:T(8,128)S(1)} %gather_fusion.1, f32[1536]{0:T(1024)S(1)} %fusion.54, pred[1536]{0:T(1024)(128)(4,1)S(1)} %and_reduce_fusion), kind=kOutput, calls=%fused_computation.6 | convolution fusion | flops 1208352768 | bytes 4201984 | tf_op jit(solution)/shard_map/jktm,kmr->kjtr/dot_general | solution.py:77
  240.4 8.4 %reduce-scatter.6.cloned.1.call-done = f32[512,128]{0,1:T(8,128)} async-done(((f32[2048,128]{0,1:T(8,128)}), f32[512,128]{0,1:T(8,128)}) %reduce-scatter.6.cloned.1.call-update) | async-done | bytes 262160 | tf_op jit(solution)/shard_map/reduce_scatter | solution.py:63
  248.7 2.5 fusion.19
  251.2 0.0 all-gather.22.cloned.1.call-start
  251.3 49.3 %all-gather.20.cloned.1.call-done = f32[4096,128]{0,1:T(8,128)} async-done(((f32[512,128]{0,1:T(8,128)}), f32[4096,128]{0,1:T(8,128)}) %all-gather.20.cloned.1.call-update) | async-done | bytes 2097168 | tf_op jit(solution)/shard_map/all_gather | solution.py:60
  300.6 4.6 %copy.65 = f32[16,8,8,512]{3,2,1,0:T(8,128)} copy(f32[16,8,8,512]{3,1,2,0:T(8,128)} %bitcast.137) | data formatting | bytes 4194304
  305.2 0.3 reduce-scatter.8.cloned.1.call-start
  305.5 23.8 %convolution_bitcast_fusion.1 = f32[2048,128]{0,1:T(8,128)} fusion(f32[8,512,2048]{2,1,0:T(8,128)} %param.8, f32[16,8,8,512]{3,2,1,0:T(8,128)} %bitcast.138), kind=kOutput, calls=%fused_computation.12 | convolution fusion | flops 12884901888 | bytes 36700160 | tf_op jit(solution)/shard_map/dot_general | solution.py:64
  329.3 0.0 all-gather.22.cloned.1.call-done
  329.3 5.4 %copy.51 = f32[8,1024,128]{2,1,0:T(8,128)} copy(f32[8,1024,128]{1,0,2:T(8,128)} %all-gather.22.cloned.1.call-done) | data formatting | bytes 8388608 | tf_op jit(solution)/shard_map/all_gather | solution.py:61
  334.7 5.0 %gather_fusion.2 = f32[1536,128]{1,0:T(8,128)S(1)} fusion(f32[8192,128]{1,0:T(8,128)} %bitcast.132, s32[2048]{0:T(1024)S(1)} %pad_clamp_fusion), kind=kCustom, calls=%fused_computation.2.clone | custom fusion | bytes 1579008 | tf_op jit(solution)/shard_map/jit(_take)/gather | solution.py:76
  339.8 4.7 %fusion = f32[16,32,128]{2,1,0:T(8,128)S(1)} fusion(f32[16,1,32,1536]{3,2,1,0:T(8,128)} %all-to-all-done, f32[1536,128]{1,0:T(8,128)S(1)} %gather_fusion.2, f32[1536]{0:T(1024)S(1)} %fusion.54, pred[1536]{0:T(1024)(128)(4,1)S(1)} %and_reduce_fusion), kind=kOutput, calls=%fused_computation.4 | convolution fusion | flops 1208352768 | bytes 4201984 | tf_op jit(solution)/shard_map/jktm,kmr->kjtr/dot_general | solution.py:77
  344.4 8.4 %reduce-scatter.8.cloned.1.call-done = f32[512,128]{0,1:T(8,128)} async-done(((f32[2048,128]{0,1:T(8,128)}), f32[512,128]{0,1:T(8,128)}) %reduce-scatter.8.cloned.1.call-update) | async-done | bytes 262160 | tf_op jit(solution)/shard_map/reduce_scatter | solution.py:63
  352.8 1.7 fusion.21
  354.6 0.8 copy.53
  355.4 0.8 copy.54
  (33 shorter events, 0.4 us)
Async XLA Ops:
  7.2 55.4 %copy-start = (f32[1,96,1536]{2,1,0:T(8,128)S(1)}, f32[1,96,1536]{2,1,0:T(8,128)}, u32[]{:S(2)}) copy-start(f32[1,96,1536]{2,1,0:T(8,128)} %param.9) | copy-start | bytes 1769476
  7.2 55.3 %all-gather.12.cloned.1.call-start = ((), (), s32[]{:S(2)}) async-start(), calls=%async_computation.4 | async-start | bytes 2359296 | tf_op jit(solution)/shard_map/all_gather | solution.py:60
  9.8 87.5 %all-gather.14.cloned.1.call-start = ((), (), s32[]{:S(2)}) async-start(), calls=%async_computation.8 | async-start | bytes 6291456 | tf_op jit(solution)/shard_map/all_gather | solution.py:61
  65.7 4.8 %copy-start.2 = (f32[8,512,128]{2,1,0:T(8,128)S(1)}, f32[8,512,128]{2,1,0:T(8,128)}, u32[]{:S(2)}) copy-start(f32[8,512,128]{2,1,0:T(8,128)} %all-gather.12.cloned.1.call-done) | copy-start | bytes 6291460
  65.7 63.9 %all-to-all-start = ((f32[16,1,32,1536]{3,2,1,0:T(8,128)}), f32[16,1,32,1536]{3,2,1,0:T(8,128)}, u32[]{:S(2)}, u32[]{:S(2)}) async-start(f32[16,1,32,1536]{3,2,1,0:T(8,128)} %convolution_bitcast_fusion), calls=%async_computation.1 | async-start | bytes 6291456 | tf_op jit(solution)/shard_map/all_to_all | solution.py:45
  70.4 24.1 %copy-start.5 = (f32[1,512,128]{2,1,0:T(8,128)S(1)}, f32[1,512,128]{2,1,0:T(8,128)}, u32[]{:S(2)}) copy-start(f32[1,512,128]{2,1,0:T(8,128)} %param.13) | copy-start | bytes 786436
  70.4 24.8 %copy-start.6 = (s32[1,1536]{1,0:T(1,128)S(1)}, s32[1,1536]{1,0:T(1,128)}, u32[]{:S(2)}) copy-start(s32[1,1536]{1,0:T(1,128)} %param.10) | copy-start | bytes 18436
  70.4 63.8 %reduce-scatter.4.cloned.1.call-start = ((), (), s32[]{:S(2)}) async-start(), calls=%async_computation.5 | async-start | bytes 1310720 | tf_op jit(solution)/shard_map/reduce_scatter | solution.py:63
  94.2 102.5 %all-gather.16.cloned.1.call-start = ((), (), s32[]{:S(2)}) async-start(), calls=%async_computation.9 | async-start | bytes 2359296 | tf_op jit(solution)/shard_map/all_gather | solution.py:60
  136.7 88.6 %all-gather.18.cloned.1.call-start = ((), (), s32[]{:S(2)}) async-start(), calls=%async_computation.10 | async-start | bytes 6291456 | tf_op jit(solution)/shard_map/all_gather | solution.py:61
  201.2 47.5 %reduce-scatter.6.cloned.1.call-start = ((), (), s32[]{:S(2)}) async-start(), calls=%async_computation.6 | async-start | bytes 1310720 | tf_op jit(solution)/shard_map/reduce_scatter | solution.py:63
  225.3 75.3 %all-gather.20.cloned.1.call-start = ((), (), s32[]{:S(2)}) async-start(), calls=%async_computation.11 | async-start | bytes 2359296 | tf_op jit(solution)/shard_map/all_gather | solution.py:60
  235.7 13.1 %copy-start.4 = (f32[512,128]{0,1:T(8,128)S(1)}, f32[512,128]{0,1:T(8,128)}, u32[]{:S(2)}) copy-start(f32[512,128]{0,1:T(8,128)} %fusion.15) | copy-start | bytes 786436
  251.2 78.1 %all-gather.22.cloned.1.call-start = ((), (), s32[]{:S(2)}) async-start(), calls=%async_computation.12 | async-start | bytes 6291456 | tf_op jit(solution)/shard_map/all_gather | solution.py:61
  305.2 47.6 %reduce-scatter.8.cloned.1.call-start = ((), (), s32[]{:S(2)}) async-start(), calls=%async_computation.7 | async-start | bytes 1310720 | tf_op jit(solution)/shard_map/reduce_scatter | solution.py:63
  334.7 21.5 %copy-start.1 = (f32[1,96,1536]{2,1,0:T(8,128)S(1)}, f32[1,96,1536]{2,1,0:T(8,128)}, u32[]{:S(2)}) copy-start(f32[1,96,1536]{2,1,0:T(8,128)} %param.9) | copy-start | bytes 1769476
  339.7 14.8 %copy-start.3 = (f32[512,128]{0,1:T(8,128)S(1)}, f32[512,128]{0,1:T(8,128)}, u32[]{:S(2)}) copy-start(f32[512,128]{0,1:T(8,128)} %fusion.19) | copy-start | bytes 786436
Sparse Core Ops, SparseCore 0:
  10.7 51.7 all-gather.11
  64.1 12.1 all-gather.13
  94.3 25.9 reduce-scatter.3
  136.8 59.7 all-gather.15
  201.3 12.1 all-gather.17
  225.4 23.2 reduce-scatter.5
  251.5 49.0 all-gather.19
  305.3 12.1 all-gather.21
  329.4 23.2 reduce-scatter.7
where the time goes:
time: 363 us
  waiting for transfers between devices  205 us (56%)
  matrix products  96.2 us (27%)
  local copies, waits for them, and re-layouts  36.5 us (10%)
  between operations  14.8 us (4%)
  starting transfers between devices  5.72 us (2%)
  other arithmetic  4.22 us (1%)
    all_gather x3, waiting for transfers between devices, on_device(): wide_panel = lax.all_gather(traces[None], 'wide', axis=0, tiled=True)  161 us
    dot_general x3, matrix products, on_device(): lax.dot_general(tile_block, stacked, (((0,), (0,)), ((), ())), precision=...  71.2 us
    all_to_all x1, waiting for transfers between devices, on_device(): lax.all_to_all(outgoing, ('wide', 'grp'), split_axis=0, concat_axis=0, ti...  27.5 us
    reduce_scatter x3, waiting for transfers between devices, on_device(): lax.psum_scatter(lax.dot_general(tile_block, stacked, (((0,), (0,)), ((),...  16.8 us
    gather x3, local copies, waits for them, and re-layouts, on_device(): jnp.take(flat_panel, interface_rows, axis=0) * live_mask[:, :, None]  14.7 us
    dot_general x3, matrix products, on_device(): jnp.einsum('jktm,kmr->kjtr', received, local_traces, precision=lax.Precis...  13.9 us
    unnamed x19, local copies, waits for them, and re-layouts  11 us
    all_gather x2, local copies, waits for them, and re-layouts, on_device(): full_panel = lax.all_gather(wide_panel[:, None], 'grp', axis=1, tiled=True)  10.8 us
  transfers between devices with their start and end apart: 10, of which 6 were waited for; matrix products, arithmetic and copies ran while one was open for 32% of the time, Pallas kernels for 0%

commit v1 on v0

--- a/solution.py
+++ b/solution.py
@@ -57,7 +57,17 @@
     traces = RELAX * row_weight * forcing
     residual = forcing
     for sweep in range(ITERS):
-        wide_panel = lax.all_gather(traces[None], "wide", axis=0, tiled=True)
+        xin = traces[None]
+        how_many = lax.axis_size("wide")
+        back = sorted(((m, (m + 1) % how_many) for m in range(how_many)))
+        w1 = xin
+        steps_seen = [w1]
+        for ix in range(1, how_many):
+            w1 = lax.ppermute(w1, "wide", back)
+            steps_seen.insert(0, w1)
+        wide_panel = jnp.roll(
+            jnp.concatenate(steps_seen, axis=0), (lax.axis_index("wide") + 1) * xin.shape[0], axis=0
+        )
         full_panel = lax.all_gather(wide_panel[:, None], "grp", axis=1, tiled=True)
         stacked = wide_panel.reshape(-1, wide_panel.shape[-1])
         boundary = lax.psum_scatter(

time: 363 us -> 399 us (1.099)
  waiting for transfers between devices: 205 us -> 224 us
  starting transfers between devices: 5.72 us -> 16.2 us
  other arithmetic: 4.22 us -> 11.2 us
  matrix products: 96.2 us -> 90.5 us
    ppermute x0 -> x21, waiting for transfers between devices: none -> 194 us  [on_device(): w1 = lax.ppermute(w1, 'wide', back)]
    all_gather x3 -> x0, waiting for transfers between devices: 161 us -> none  [on_device(): wide_panel = lax.all_gather(traces[None], 'wide', axis=0, tiled=True)]
    ppermute x0 -> x21, starting transfers between devices: none -> 9.44 us  [on_device(): w1 = lax.ppermute(w1, 'wide', back)]
    all_to_all x1, waiting for transfers between devices: 27.5 us -> 19.3 us  [on_device(): lax.all_to_all(outgoing, ('wide', 'grp'), split_axis=0, concat_axis=0, ti...]
    reduce_scatter x3, waiting for transfers between devices: 16.8 us -> 10 us  [on_device(): lax.psum_scatter(lax.dot_general(tile_block, stacked, (((0,), (0,)), ((),...]
    all_gather x2 -> x3, local copies, waits for them, and re-layouts: 10.8 us -> 16.9 us  [on_device(): full_panel = lax.all_gather(wide_panel[:, None], 'grp', axis=1, tiled=True)]
    concatenate x0 -> x4, other arithmetic: none -> 5.67 us  [the longest x3 5.65 us: on_device(): jnp.roll(jnp.concatenate(steps_seen, axis=0), (lax.axis_index('wide') + 1...]
    dot_general x3, matrix products: 6.67 us -> 2.4 us  [on_device(): jnp.einsum('kjti,kjtr->ir', placement, values, precision=lax.Precision.HI...]
  transfers between devices with their start and end apart: 10 -> 28, of which waited for: 6 -> 23; matrix products, arithmetic and copies ran while one was open for 32% -> 32% of each run, Pallas kernels for 0% -> 0%
where the time goes in v1:
time: 399 us; the launch traced here: 398 us
  waiting for transfers between devices  224 us (56%)
  matrix products  90.5 us (23%)
  local copies, waits for them, and re-layouts  39.2 us (10%)
  between operations  16.6 us (4%)
  starting transfers between devices  16.2 us (4%)
  other arithmetic  11.2 us (3%)
    ppermute x21, waiting for transfers between devices, on_device(): w1 = lax.ppermute(w1, 'wide', back)  194 us
    dot_general x3, matrix products, on_device(): lax.dot_general(tile_block, stacked, (((0,), (0,)), ((), ())), precision=...  69.6 us
    all_to_all x1, waiting for transfers between devices, on_device(): lax.all_to_all(outgoing, ('wide', 'grp'), split_axis=0, concat_axis=0, ti...  19.3 us
    all_gather x3, local copies, waits for them, and re-layouts, on_device(): full_panel = lax.all_gather(wide_panel[:, None], 'grp', axis=1, tiled=True)  16.9 us
    gather x3, local copies, waits for them, and re-layouts, on_device(): jnp.take(flat_panel, interface_rows, axis=0) * live_mask[:, :, None]  14.4 us
    dot_general x3, matrix products, on_device(): jnp.einsum('jktm,kmr->kjtr', received, local_traces, precision=lax.Precis...  14.2 us
    reduce_scatter x3, waiting for transfers between devices, on_device(): lax.psum_scatter(lax.dot_general(tile_block, stacked, (((0,), (0,)), ((),...  10 us
    ppermute x21, starting transfers between devices, on_device(): w1 = lax.ppermute(w1, 'wide', back)  9.44 us
  transfers between devices with their start and end apart: 28, of which 23 were waited for; matrix products, arithmetic and copies ran while one was open for 32% of the time, Pallas kernels for 0%

profile of v1, /device:TPU:0, one launch (start us, length us, event | category | flops | bytes accessed | tf_op | source)
XLA Modules:
  0.0 397.7 jit_solution(394294983996259930)
XLA Ops:
  8.0 1.1 copy.36
  9.9 3.0 collective-permute-start
  12.9 9.3 %collective-permute-done = f32[1,512,128]{1,2,0:T(8,128)S(1)} collective-permute-done((f32[1,512,128]{1,2,0:T(8,128)S(1)}, f32[1,512,128]{1,2,0:T(8,128)S(1)}, u32[]{:S(2)}, u32[]{:S(2)}) %collective-permute-start) | collective-permute-done | bytes 262176 | tf_op jit(solution)/shard_map/ppermute | solution.py:66
  22.3 10.2 %collective-permute-done.1 = f32[1,512,128]{1,2,0:T(8,128)S(1)} collective-permute-done((f32[1,512,128]{1,2,0:T(8,128)S(1)}, f32[1,512,128]{1,2,0:T(8,128)S(1)}, u32[]{:S(2)}, u32[]{:S(2)}) %collective-permute-start.1) | collective-permute-done | bytes 262176 | tf_op jit(solution)/shard_map/ppermute | solution.py:66
  32.4 9.3 %collective-permute-done.2 = f32[1,512,128]{1,2,0:T(8,128)S(1)} collective-permute-done((f32[1,512,128]{1,2,0:T(8,128)S(1)}, f32[1,512,128]{1,2,0:T(8,128)S(1)}, u32[]{:S(2)}, u32[]{:S(2)}) %collective-permute-start.2) | collective-permute-done | bytes 262176 | tf_op jit(solution)/shard_map/ppermute | solution.py:66
  41.7 9.1 %collective-permute-done.3 = f32[1,512,128]{1,2,0:T(8,128)S(1)} collective-permute-done((f32[1,512,128]{1,2,0:T(8,128)S(1)}, f32[1,512,128]{1,2,0:T(8,128)S(1)}, u32[]{:S(2)}, u32[]{:S(2)}) %collective-permute-start.3) | collective-permute-done | bytes 262176 | tf_op jit(solution)/shard_map/ppermute | solution.py:66
  51.6 8.3 %collective-permute-done.4 = f32[1,512,128]{1,2,0:T(8,128)S(1)} collective-permute-done((f32[1,512,128]{1,2,0:T(8,128)S(1)}, f32[1,512,128]{1,2,0:T(8,128)S(1)}, u32[]{:S(2)}, u32[]{:S(2)}) %collective-permute-start.4) | collective-permute-done | bytes 262176 | tf_op jit(solution)/shard_map/ppermute | solution.py:66
  60.1 9.5 %collective-permute-done.5 = f32[1,512,128]{1,2,0:T(8,128)S(1)} collective-permute-done((f32[1,512,128]{1,2,0:T(8,128)S(1)}, f32[1,512,128]{1,2,0:T(8,128)S(1)}, u32[]{:S(2)}, u32[]{:S(2)}) %collective-permute-start.5) | collective-permute-done | bytes 262176 | tf_op jit(solution)/shard_map/ppermute | solution.py:66
  69.6 3.1 convolution_bitcast_fusion
  72.7 6.1 %all-to-all-start = ((f32[16,1,32,1536]{3,2,1,0:T(8,128)}), f32[16,1,32,1536]{3,2,1,0:T(8,128)}, u32[]{:S(2)}, u32[]{:S(2)}) async-start(f32[16,1,32,1536]{3,2,1,0:T(8,128)} %convolution_bitcast_fusion), calls=%async_computation.1 | async-start | bytes 6291456 | tf_op jit(solution)/shard_map/all_to_all | solution.py:45
  79.1 1.9 fusion.9
  81.1 1.5 copy-done.2
  82.6 22.5 %convolution_bitcast_fusion.3 = f32[2048,128]{0,1:T(8,128)} fusion(f32[8,512,128]{1,2,0:T(8,128)S(1)} %copy-done.2, f32[8,512,2048]{2,1,0:T(8,128)} %param.10), kind=kOutput, calls=%fused_computation.20 | convolution fusion | flops 12884901888 | bytes 36700160 | tf_op jit(solution)/shard_map/dot_general | solution.py:74
  106.9 1.2 fusion.6
  108.2 5.8 %copy.39 = f32[8,1024,128]{2,1,0:T(8,128)} copy(f32[8,1024,128]{1,2,0:T(8,128)} %all-gather.7.cloned.1.call-done) | data formatting | bytes 8388608 | tf_op jit(solution)/shard_map/all_gather | solution.py:71
  114.0 4.9 %gather_fusion = f32[1536,128]{1,0:T(8,128)S(1)} fusion(f32[8192,128]{1,0:T(8,128)} %bitcast.116, s32[2048]{0:T(1024)S(1)} %pad_clamp_fusion), kind=kCustom, calls=%fused_computation.clone | custom fusion | bytes 1579008 | tf_op jit(solution)/shard_map/jit(_take)/gather | solution.py:86
  118.8 19.3 %all-to-all-done = f32[16,1,32,1536]{3,2,1,0:T(8,128)} async-done(((f32[16,1,32,1536]{3,2,1,0:T(8,128)}), f32[16,1,32,1536]{3,2,1,0:T(8,128)}, u32[]{:S(2)}, u32[]{:S(2)}) %all-to-all-start) | async-done | bytes 3145760 | tf_op jit(solution)/shard_map/all_to_all | solution.py:45
  138.1 4.6 %fusion.4 = f32[16,32,128]{2,1,0:T(8,128)S(1)} fusion(f32[16,1,32,1536]{3,2,1,0:T(8,128)} %all-to-all-done, f32[1536,128]{1,0:T(8,128)S(1)} %gather_fusion, f32[1536]{0:T(1024)S(1)} %fusion.47, pred[1536]{0:T(1024)(128)(4,1)S(1)} %and_reduce_fusion), kind=kOutput, calls=%fused_computation.14 | convolution fusion | flops 1208352768 | bytes 4201984 | tf_op jit(solution)/shard_map/jktm,kmr->kjtr/dot_general | solution.py:87
  144.6 4.8 %collective-permute-start.7 = (f32[1,512,128]{1,2,0:T(8,128)S(1)}, f32[1,512,128]{1,2,0:T(8,128)S(1)}, u32[]{:S(2)}, u32[]{:S(2)}) collective-permute-start(f32[1,512,128]{1,2,0:T(8,128)S(1)} %fusion.43), channel_id=1, source_target_pairs={{0,4},{4,8},{8,12},{12,16},{16,20},{20,24},{24,28},{28,0},{1,5},{5... | collective-permute-start | bytes 786440 | tf_op jit(solution)/shard_map/ppermute | solution.py:66
  149.5 16.1 %collective-permute-done.7 = f32[1,512,128]{1,2,0:T(8,128)S(1)} collective-permute-done((f32[1,512,128]{1,2,0:T(8,128)S(1)}, f32[1,512,128]{1,2,0:T(8,128)S(1)}, u32[]{:S(2)}, u32[]{:S(2)}) %collective-permute-start.7) | collective-permute-done | bytes 262176 | tf_op jit(solution)/shard_map/ppermute | solution.py:66
  165.6 10.7 %collective-permute-done.8 = f32[1,512,128]{1,2,0:T(8,128)S(1)} collective-permute-done((f32[1,512,128]{1,2,0:T(8,128)S(1)}, f32[1,512,128]{1,2,0:T(8,128)S(1)}, u32[]{:S(2)}, u32[]{:S(2)}) %collective-permute-start.8) | collective-permute-done | bytes 262176 | tf_op jit(solution)/shard_map/ppermute | solution.py:66
  176.3 9.9 %collective-permute-done.9 = f32[1,512,128]{1,2,0:T(8,128)S(1)} collective-permute-done((f32[1,512,128]{1,2,0:T(8,128)S(1)}, f32[1,512,128]{1,2,0:T(8,128)S(1)}, u32[]{:S(2)}, u32[]{:S(2)}) %collective-permute-start.9) | collective-permute-done | bytes 262176 | tf_op jit(solution)/shard_map/ppermute | solution.py:66
  186.2 9.1 %collective-permute-done.10 = f32[1,512,128]{1,2,0:T(8,128)S(1)} collective-permute-done((f32[1,512,128]{1,2,0:T(8,128)S(1)}, f32[1,512,128]{1,2,0:T(8,128)S(1)}, u32[]{:S(2)}, u32[]{:S(2)}) %collective-permute-start.10) | collective-permute-done | bytes 262176 | tf_op jit(solution)/shard_map/ppermute | solution.py:66
  195.3 9.1 %collective-permute-done.11 = f32[1,512,128]{1,2,0:T(8,128)S(1)} collective-permute-done((f32[1,512,128]{1,2,0:T(8,128)S(1)}, f32[1,512,128]{1,2,0:T(8,128)S(1)}, u32[]{:S(2)}, u32[]{:S(2)}) %collective-permute-start.11) | collective-permute-done | bytes 262176 | tf_op jit(solution)/shard_map/ppermute | solution.py:66
  204.3 9.1 %collective-permute-done.12 = f32[1,512,128]{1,2,0:T(8,128)S(1)} collective-permute-done((f32[1,512,128]{1,2,0:T(8,128)S(1)}, f32[1,512,128]{1,2,0:T(8,128)S(1)}, u32[]{:S(2)}, u32[]{:S(2)}) %collective-permute-start.12) | collective-permute-done | bytes 262176 | tf_op jit(solution)/shard_map/ppermute | solution.py:66
  213.4 9.1 %collective-permute-done.13 = f32[1,512,128]{1,2,0:T(8,128)S(1)} collective-permute-done((f32[1,512,128]{1,2,0:T(8,128)S(1)}, f32[1,512,128]{1,2,0:T(8,128)S(1)}, u32[]{:S(2)}, u32[]{:S(2)}) %collective-permute-start.13) | collective-permute-done | bytes 262176 | tf_op jit(solution)/shard_map/ppermute | solution.py:66
  222.7 1.9 fusion.8
  224.7 1.5 copy-done.3
  226.2 23.4 %convolution_bitcast_fusion.2 = f32[2048,128]{0,1:T(8,128)} fusion(f32[8,512,128]{1,2,0:T(8,128)S(1)} %copy-done.3, f32[8,512,2048]{2,1,0:T(8,128)} %param.10), kind=kOutput, calls=%fused_computation.19 | convolution fusion | flops 12884901888 | bytes 36700160 | tf_op jit(solution)/shard_map/dot_general | solution.py:74
  249.9 5.5 %copy.41 = f32[8,1024,128]{2,1,0:T(8,128)} copy(f32[8,1024,128]{1,2,0:T(8,128)} %all-gather.9.cloned.1.call-done) | data formatting | bytes 8388608 | tf_op jit(solution)/shard_map/all_gather | solution.py:71
  255.4 4.8 %gather_fusion.1 = f32[1536,128]{1,0:T(8,128)S(1)} fusion(f32[8192,128]{1,0:T(8,128)} %bitcast.117, s32[2048]{0:T(1024)S(1)} %pad_clamp_fusion), kind=kCustom, calls=%fused_computation.1.clone | custom fusion | bytes 1579008 | tf_op jit(solution)/shard_map/jit(_take)/gather | solution.py:86
  260.2 4.7 %fusion.2 = f32[16,32,128]{2,1,0:T(8,128)S(1)} fusion(f32[16,1,32,1536]{3,2,1,0:T(8,128)} %all-to-all-done, f32[1536,128]{1,0:T(8,128)S(1)} %gather_fusion.1, f32[1536]{0:T(1024)S(1)} %fusion.47, pred[1536]{0:T(1024)(128)(4,1)S(1)} %and_reduce_fusion), kind=kOutput, calls=%fused_computation.12 | convolution fusion | flops 1208352768 | bytes 4201984 | tf_op jit(solution)/shard_map/jktm,kmr->kjtr/dot_general | solution.py:87
  265.7 5.6 %reduce-scatter.6.cloned.1.call-done = f32[512,128]{0,1:T(8,128)} async-done(((f32[2048,128]{0,1:T(8,128)}), f32[512,128]{0,1:T(8,128)}) %reduce-scatter.6.cloned.1.call-update) | async-done | bytes 262160 | tf_op jit(solution)/shard_map/reduce_scatter | solution.py:73
  272.4 1.5 collective-permute-start.14
  273.9 9.0 %collective-permute-done.14 = f32[1,512,128]{1,2,0:T(8,128)S(1)} collective-permute-done((f32[1,512,128]{1,2,0:T(8,128)S(1)}, f32[1,512,128]{1,2,0:T(8,128)S(1)}, u32[]{:S(2)}, u32[]{:S(2)}) %collective-permute-start.14) | collective-permute-done | bytes 262176 | tf_op jit(solution)/shard_map/ppermute | solution.py:66
  282.9 9.6 %collective-permute-done.15 = f32[1,512,128]{1,2,0:T(8,128)S(1)} collective-permute-done((f32[1,512,128]{1,2,0:T(8,128)S(1)}, f32[1,512,128]{1,2,0:T(8,128)S(1)}, u32[]{:S(2)}, u32[]{:S(2)}) %collective-permute-start.15) | collective-permute-done | bytes 262176 | tf_op jit(solution)/shard_map/ppermute | solution.py:66
  292.5 9.1 %collective-permute-done.16 = f32[1,512,128]{1,2,0:T(8,128)S(1)} collective-permute-done((f32[1,512,128]{1,2,0:T(8,128)S(1)}, f32[1,512,128]{1,2,0:T(8,128)S(1)}, u32[]{:S(2)}, u32[]{:S(2)}) %collective-permute-start.16) | collective-permute-done | bytes 262176 | tf_op jit(solution)/shard_map/ppermute | solution.py:66
  301.6 9.1 %collective-permute-done.17 = f32[1,512,128]{1,2,0:T(8,128)S(1)} collective-permute-done((f32[1,512,128]{1,2,0:T(8,128)S(1)}, f32[1,512,128]{1,2,0:T(8,128)S(1)}, u32[]{:S(2)}, u32[]{:S(2)}) %collective-permute-start.17) | collective-permute-done | bytes 262176 | tf_op jit(solution)/shard_map/ppermute | solution.py:66
  310.7 9.4 %collective-permute-done.18 = f32[1,512,128]{1,2,0:T(8,128)S(1)} collective-permute-done((f32[1,512,128]{1,2,0:T(8,128)S(1)}, f32[1,512,128]{1,2,0:T(8,128)S(1)}, u32[]{:S(2)}, u32[]{:S(2)}) %collective-permute-start.18) | collective-permute-done | bytes 262176 | tf_op jit(solution)/shard_map/ppermute | solution.py:66
  320.0 10.5 %collective-permute-done.19 = f32[1,512,128]{1,2,0:T(8,128)S(1)} collective-permute-done((f32[1,512,128]{1,2,0:T(8,128)S(1)}, f32[1,512,128]{1,2,0:T(8,128)S(1)}, u32[]{:S(2)}, u32[]{:S(2)}) %collective-permute-start.19) | collective-permute-done | bytes 262176 | tf_op jit(solution)/shard_map/ppermute | solution.py:66
  330.5 9.1 %collective-permute-done.20 = f32[1,512,128]{1,2,0:T(8,128)S(1)} collective-permute-done((f32[1,512,128]{1,2,0:T(8,128)S(1)}, f32[1,512,128]{1,2,0:T(8,128)S(1)}, u32[]{:S(2)}, u32[]{:S(2)}) %collective-permute-start.20) | collective-permute-done | bytes 262176 | tf_op jit(solution)/shard_map/ppermute | solution.py:66
  339.8 1.9 fusion.7
  341.8 1.5 copy-done.4
  343.3 23.7 %convolution_bitcast_fusion.1 = f32[2048,128]{0,1:T(8,128)} fusion(f32[8,512,128]{1,2,0:T(8,128)S(1)} %copy-done.4, f32[8,512,2048]{2,1,0:T(8,128)} %param.10), kind=kOutput, calls=%fused_computation.18 | convolution fusion | flops 12884901888 | bytes 36700160 | tf_op jit(solution)/shard_map/dot_general | solution.py:74
  367.0 5.7 %copy.43 = f32[8,1024,128]{2,1,0:T(8,128)} copy(f32[8,1024,128]{1,2,0:T(8,128)} %all-gather.11.cloned.1.call-done) | data formatting | bytes 8388608 | tf_op jit(solution)/shard_map/all_gather | solution.py:71
  372.7 4.8 %gather_fusion.2 = f32[1536,128]{1,0:T(8,128)S(1)} fusion(f32[8192,128]{1,0:T(8,128)} %bitcast.115, s32[2048]{0:T(1024)S(1)} %pad_clamp_fusion), kind=kCustom, calls=%fused_computation.2.clone | custom fusion | bytes 1579008 | tf_op jit(solution)/shard_map/jit(_take)/gather | solution.py:86
  377.5 4.9 %fusion = f32[16,32,128]{2,1,0:T(8,128)S(1)} fusion(f32[16,1,32,1536]{3,2,1,0:T(8,128)} %all-to-all-done, f32[1536,128]{1,0:T(8,128)S(1)} %gather_fusion.2, f32[1536]{0:T(1024)S(1)} %fusion.47, pred[1536]{0:T(1024)(128)(4,1)S(1)} %and_reduce_fusion), kind=kOutput, calls=%fused_computation.10 | convolution fusion | flops 1208352768 | bytes 4201984 | tf_op jit(solution)/shard_map/jktm,kmr->kjtr/dot_general | solution.py:87
  383.2 4.5 %reduce-scatter.8.cloned.1.call-done = f32[512,128]{0,1:T(8,128)} async-done(((f32[2048,128]{0,1:T(8,128)}), f32[512,128]{0,1:T(8,128)}) %reduce-scatter.8.cloned.1.call-update) | async-done | bytes 262160 | tf_op jit(solution)/shard_map/reduce_scatter | solution.py:73
  (100 shorter events, 11.1 us)
Async XLA Ops:
  8.0 61.6 %copy-start = (f32[1,96,1536]{2,1,0:T(8,128)S(1)}, f32[1,96,1536]{2,1,0:T(8,128)}, u32[]{:S(2)}) copy-start(f32[1,96,1536]{2,1,0:T(8,128)} %param.11) | copy-start | bytes 1769476
  9.9 12.4 %collective-permute-start = (f32[1,512,128]{1,2,0:T(8,128)S(1)}, f32[1,512,128]{1,2,0:T(8,128)S(1)}, u32[]{:S(2)}, u32[]{:S(2)}) collective-permute-start(f32[1,512,128]{1,2,0:T(8,128)S(1)} %broadcast_multiply_fusion), channel_id=1, source_target_pairs={{0,4},{4,8},{8,12},{12,16},{16,20},{20,24},{24,28},{28,0},{1,5},{5... | collective-permute-start | bytes 786440 | tf_op jit(solution)/shard_map/ppermute | solution.py:66
  22.3 10.2 %collective-permute-start.1 = (f32[1,512,128]{1,2,0:T(8,128)S(1)}, f32[1,512,128]{1,2,0:T(8,128)S(1)}, u32[]{:S(2)}, u32[]{:S(2)}) collective-permute-start(f32[1,512,128]{1,2,0:T(8,128)S(1)} %collective-permute-done), channel_id=1, source_target_pairs={{0,4},{4,8},{8,12},{12,16},{16,20},{20,24},{24,28},{28,0},{1,5},{5... | collective-permute-start | bytes 786440 | tf_op jit(solution)/shard_map/ppermute | solution.py:66
  32.4 9.3 %collective-permute-start.2 = (f32[1,512,128]{1,2,0:T(8,128)S(1)}, f32[1,512,128]{1,2,0:T(8,128)S(1)}, u32[]{:S(2)}, u32[]{:S(2)}) collective-permute-start(f32[1,512,128]{1,2,0:T(8,128)S(1)} %collective-permute-done.1), channel_id=1, source_target_pairs={{0,4},{4,8},{8,12},{12,16},{16,20},{20,24},{24,28},{28,0},{1,5},{5... | collective-permute-start | bytes 786440 | tf_op jit(solution)/shard_map/ppermute | solution.py:66
  41.7 9.1 %collective-permute-start.3 = (f32[1,512,128]{1,2,0:T(8,128)S(1)}, f32[1,512,128]{1,2,0:T(8,128)S(1)}, u32[]{:S(2)}, u32[]{:S(2)}) collective-permute-start(f32[1,512,128]{1,2,0:T(8,128)S(1)} %collective-permute-done.2), channel_id=1, source_target_pairs={{0,4},{4,8},{8,12},{12,16},{16,20},{20,24},{24,28},{28,0},{1,5},{5... | collective-permute-start | bytes 786440 | tf_op jit(solution)/shard_map/ppermute | solution.py:66
  50.8 9.1 %collective-permute-start.4 = (f32[1,512,128]{1,2,0:T(8,128)S(1)}, f32[1,512,128]{1,2,0:T(8,128)S(1)}, u32[]{:S(2)}, u32[]{:S(2)}) collective-permute-start(f32[1,512,128]{1,2,0:T(8,128)S(1)} %collective-permute-done.3), channel_id=1, source_target_pairs={{0,4},{4,8},{8,12},{12,16},{16,20},{20,24},{24,28},{28,0},{1,5},{5... | collective-permute-start | bytes 786440 | tf_op jit(solution)/shard_map/ppermute | solution.py:66
  59.9 9.7 %collective-permute-start.5 = (f32[1,512,128]{1,2,0:T(8,128)S(1)}, f32[1,512,128]{1,2,0:T(8,128)S(1)}, u32[]{:S(2)}, u32[]{:S(2)}) collective-permute-start(f32[1,512,128]{1,2,0:T(8,128)S(1)} %collective-permute-done.4), channel_id=1, source_target_pairs={{0,4},{4,8},{8,12},{12,16},{16,20},{20,24},{24,28},{28,0},{1,5},{5... | collective-permute-start | bytes 786440 | tf_op jit(solution)/shard_map/ppermute | solution.py:66
  69.6 9.3 %collective-permute-start.6 = (f32[1,512,128]{1,2,0:T(8,128)S(1)}, f32[1,512,128]{1,2,0:T(8,128)S(1)}, u32[]{:S(2)}, u32[]{:S(2)}) collective-permute-start(f32[1,512,128]{1,2,0:T(8,128)S(1)} %collective-permute-done.5), channel_id=1, source_target_pairs={{0,4},{4,8},{8,12},{12,16},{16,20},{20,24},{24,28},{28,0},{1,5},{5... | collective-permute-start | bytes 786440 | tf_op jit(solution)/shard_map/ppermute | solution.py:66
  72.7 65.4 %all-to-all-start = ((f32[16,1,32,1536]{3,2,1,0:T(8,128)}), f32[16,1,32,1536]{3,2,1,0:T(8,128)}, u32[]{:S(2)}, u32[]{:S(2)}) async-start(f32[16,1,32,1536]{3,2,1,0:T(8,128)} %convolution_bitcast_fusion), calls=%async_computation.1 | async-start | bytes 6291456 | tf_op jit(solution)/shard_map/all_to_all | solution.py:45
  78.8 29.3 %all-gather.7.cloned.1.call-start = ((), (), s32[]{:S(2)}) async-start(), calls=%async_computation.7 | async-start | bytes 6291456 | tf_op jit(solution)/shard_map/all_gather | solution.py:71
  81.0 1.6 copy-start.2
  81.1 24.3 %copy-start.9 = (s32[1,1536]{1,0:T(1,128)S(1)}, s32[1,1536]{1,0:T(1,128)}, u32[]{:S(2)}) copy-start(s32[1,1536]{1,0:T(1,128)} %param.12) | copy-start | bytes 18436
  81.1 62.5 %reduce-scatter.4.cloned.1.call-start = ((), (), s32[]{:S(2)}) async-start(), calls=%async_computation.4 | async-start | bytes 1310720 | tf_op jit(solution)/shard_map/reduce_scatter | solution.py:73
  105.2 144.7 %all-gather.9.cloned.1.call-start = ((), (), s32[]{:S(2)}) async-start(), calls=%async_computation.8 | async-start | bytes 6291456 | tf_op jit(solution)/shard_map/all_gather | solution.py:71
  108.1 34.6 %copy-start.5 = (f32[16,32,512]{2,1,0:T(8,128)}, f32[16,32,512]{2,1,0:T(8,128)S(1)}, u32[]{:S(2)}) copy-start(f32[16,32,512]{2,1,0:T(8,128)S(1)} %fusion.6) | copy-start | bytes 3145732
  144.6 21.0 %collective-permute-start.7 = (f32[1,512,128]{1,2,0:T(8,128)S(1)}, f32[1,512,128]{1,2,0:T(8,128)S(1)}, u32[]{:S(2)}, u32[]{:S(2)}) collective-permute-start(f32[1,512,128]{1,2,0:T(8,128)S(1)} %fusion.43), channel_id=1, source_target_pairs={{0,4},{4,8},{8,12},{12,16},{16,20},{20,24},{24,28},{28,0},{1,5},{5... | collective-permute-start | bytes 786440 | tf_op jit(solution)/shard_map/ppermute | solution.py:66
  165.6 10.7 %collective-permute-start.8 = (f32[1,512,128]{1,2,0:T(8,128)S(1)}, f32[1,512,128]{1,2,0:T(8,128)S(1)}, u32[]{:S(2)}, u32[]{:S(2)}) collective-permute-start(f32[1,512,128]{1,2,0:T(8,128)S(1)} %collective-permute-done.7), channel_id=1, source_target_pairs={{0,4},{4,8},{8,12},{12,16},{16,20},{20,24},{24,28},{28,0},{1,5},{5... | collective-permute-start | bytes 786440 | tf_op jit(solution)/shard_map/ppermute | solution.py:66
  176.3 9.9 %collective-permute-start.9 = (f32[1,512,128]{1,2,0:T(8,128)S(1)}, f32[1,512,128]{1,2,0:T(8,128)S(1)}, u32[]{:S(2)}, u32[]{:S(2)}) collective-permute-start(f32[1,512,128]{1,2,0:T(8,128)S(1)} %collective-permute-done.8), channel_id=1, source_target_pairs={{0,4},{4,8},{8,12},{12,16},{16,20},{20,24},{24,28},{28,0},{1,5},{5... | collective-permute-start | bytes 786440 | tf_op jit(solution)/shard_map/ppermute | solution.py:66
  186.2 9.1 %collective-permute-start.10 = (f32[1,512,128]{1,2,0:T(8,128)S(1)}, f32[1,512,128]{1,2,0:T(8,128)S(1)}, u32[]{:S(2)}, u32[]{:S(2)}) collective-permute-start(f32[1,512,128]{1,2,0:T(8,128)S(1)} %collective-permute-done.9), channel_id=1, source_target_pairs={{0,4},{4,8},{8,12},{12,16},{16,20},{20,24},{24,28},{28,0},{1,5},{5... | collective-permute-start | bytes 786440 | tf_op jit(solution)/shard_map/ppermute | solution.py:66
  195.3 9.1 %collective-permute-start.11 = (f32[1,512,128]{1,2,0:T(8,128)S(1)}, f32[1,512,128]{1,2,0:T(8,128)S(1)}, u32[]{:S(2)}, u32[]{:S(2)}) collective-permute-start(f32[1,512,128]{1,2,0:T(8,128)S(1)} %collective-permute-done.10), channel_id=1, source_target_pairs={{0,4},{4,8},{8,12},{12,16},{16,20},{20,24},{24,28},{28,0},{1,5},{5... | collective-permute-start | bytes 786440 | tf_op jit(solution)/shard_map/ppermute | solution.py:66
  204.3 9.1 %collective-permute-start.12 = (f32[1,512,128]{1,2,0:T(8,128)S(1)}, f32[1,512,128]{1,2,0:T(8,128)S(1)}, u32[]{:S(2)}, u32[]{:S(2)}) collective-permute-start(f32[1,512,128]{1,2,0:T(8,128)S(1)} %collective-permute-done.11), channel_id=1, source_target_pairs={{0,4},{4,8},{8,12},{12,16},{16,20},{20,24},{24,28},{28,0},{1,5},{5... | collective-permute-start | bytes 786440 | tf_op jit(solution)/shard_map/ppermute | solution.py:66
  213.4 9.1 %collective-permute-start.13 = (f32[1,512,128]{1,2,0:T(8,128)S(1)}, f32[1,512,128]{1,2,0:T(8,128)S(1)}, u32[]{:S(2)}, u32[]{:S(2)}) collective-permute-start(f32[1,512,128]{1,2,0:T(8,128)S(1)} %collective-permute-done.12), channel_id=1, source_target_pairs={{0,4},{4,8},{8,12},{12,16},{16,20},{20,24},{24,28},{28,0},{1,5},{5... | collective-permute-start | bytes 786440 | tf_op jit(solution)/shard_map/ppermute | solution.py:66
  224.6 1.6 copy-start.3
  224.6 46.6 %reduce-scatter.6.cloned.1.call-start = ((), (), s32[]{:S(2)}) async-start(), calls=%async_computation.5 | async-start | bytes 1310720 | tf_op jit(solution)/shard_map/reduce_scatter | solution.py:73
  249.6 117.4 %all-gather.11.cloned.1.call-start = ((), (), s32[]{:S(2)}) async-start(), calls=%async_computation.9 | async-start | bytes 6291456 | tf_op jit(solution)/shard_map/all_gather | solution.py:71
  260.2 4.7 %copy-start.6 = (f32[16,32,512]{2,1,0:T(8,128)S(1)}, f32[16,32,512]{2,1,0:T(8,128)}, u32[]{:S(2)}) copy-start(f32[16,32,512]{2,1,0:T(8,128)} %copy-done.5) | copy-start | bytes 3145732
  260.2 11.1 %copy-start.8 = (f32[512,128]{0,1:T(8,128)S(1)}, f32[512,128]{0,1:T(8,128)}, u32[]{:S(2)}) copy-start(f32[512,128]{0,1:T(8,128)} %reduce-scatter.4.cloned.1.call-done) | copy-start | bytes 786436
  272.4 10.5 %collective-permute-start.14 = (f32[1,512,128]{1,2,0:T(8,128)S(1)}, f32[1,512,128]{1,2,0:T(8,128)S(1)}, u32[]{:S(2)}, u32[]{:S(2)}) collective-permute-start(f32[1,512,128]{1,2,0:T(8,128)S(1)} %bitcast.118), channel_id=1, source_target_pairs={{0,4},{4,8},{8,12},{12,16},{16,20},{20,24},{24,28},{28,0},{1,5},{5... | collective-permute-start | bytes 786440 | tf_op jit(solution)/shard_map/ppermute | solution.py:66
  282.9 9.6 %collective-permute-start.15 = (f32[1,512,128]{1,2,0:T(8,128)S(1)}, f32[1,512,128]{1,2,0:T(8,128)S(1)}, u32[]{:S(2)}, u32[]{:S(2)}) collective-permute-start(f32[1,512,128]{1,2,0:T(8,128)S(1)} %collective-permute-done.14), channel_id=1, source_target_pairs={{0,4},{4,8},{8,12},{12,16},{16,20},{20,24},{24,28},{28,0},{1,5},{5... | collective-permute-start | bytes 786440 | tf_op jit(solution)/shard_map/ppermute | solution.py:66
  292.5 9.1 %collective-permute-start.16 = (f32[1,512,128]{1,2,0:T(8,128)S(1)}, f32[1,512,128]{1,2,0:T(8,128)S(1)}, u32[]{:S(2)}, u32[]{:S(2)}) collective-permute-start(f32[1,512,128]{1,2,0:T(8,128)S(1)} %collective-permute-done.15), channel_id=1, source_target_pairs={{0,4},{4,8},{8,12},{12,16},{16,20},{20,24},{24,28},{28,0},{1,5},{5... | collective-permute-start | bytes 786440 | tf_op jit(solution)/shard_map/ppermute | solution.py:66
  301.6 9.1 %collective-permute-start.17 = (f32[1,512,128]{1,2,0:T(8,128)S(1)}, f32[1,512,128]{1,2,0:T(8,128)S(1)}, u32[]{:S(2)}, u32[]{:S(2)}) collective-permute-start(f32[1,512,128]{1,2,0:T(8,128)S(1)} %collective-permute-done.16), channel_id=1, source_target_pairs={{0,4},{4,8},{8,12},{12,16},{16,20},{20,24},{24,28},{28,0},{1,5},{5... | collective-permute-start | bytes 786440 | tf_op jit(solution)/shard_map/ppermute | solution.py:66
  310.7 9.4 %collective-permute-start.18 = (f32[1,512,128]{1,2,0:T(8,128)S(1)}, f32[1,512,128]{1,2,0:T(8,128)S(1)}, u32[]{:S(2)}, u32[]{:S(2)}) collective-permute-start(f32[1,512,128]{1,2,0:T(8,128)S(1)} %collective-permute-done.17), channel_id=1, source_target_pairs={{0,4},{4,8},{8,12},{12,16},{16,20},{20,24},{24,28},{28,0},{1,5},{5... | collective-permute-start | bytes 786440 | tf_op jit(solution)/shard_map/ppermute | solution.py:66
  320.0 10.5 %collective-permute-start.19 = (f32[1,512,128]{1,2,0:T(8,128)S(1)}, f32[1,512,128]{1,2,0:T(8,128)S(1)}, u32[]{:S(2)}, u32[]{:S(2)}) collective-permute-start(f32[1,512,128]{1,2,0:T(8,128)S(1)} %collective-permute-done.18), channel_id=1, source_target_pairs={{0,4},{4,8},{8,12},{12,16},{16,20},{20,24},{24,28},{28,0},{1,5},{5... | collective-permute-start | bytes 786440 | tf_op jit(solution)/shard_map/ppermute | solution.py:66
  330.5 9.1 %collective-permute-start.20 = (f32[1,512,128]{1,2,0:T(8,128)S(1)}, f32[1,512,128]{1,2,0:T(8,128)S(1)}, u32[]{:S(2)}, u32[]{:S(2)}) collective-permute-start(f32[1,512,128]{1,2,0:T(8,128)S(1)} %collective-permute-done.19), channel_id=1, source_target_pairs={{0,4},{4,8},{8,12},{12,16},{16,20},{20,24},{24,28},{28,0},{1,5},{5... | collective-permute-start | bytes 786440 | tf_op jit(solution)/shard_map/ppermute | solution.py:66
  341.7 1.6 copy-start.4
  341.7 45.9 %reduce-scatter.8.cloned.1.call-start = ((), (), s32[]{:S(2)}) async-start(), calls=%async_computation.6 | async-start | bytes 1310720 | tf_op jit(solution)/shard_map/reduce_scatter | solution.py:73
  377.5 4.9 %copy-start.7 = (f32[16,32,512]{2,1,0:T(8,128)S(1)}, f32[16,32,512]{2,1,0:T(8,128)}, u32[]{:S(2)}) copy-start(f32[16,32,512]{2,1,0:T(8,128)} %copy-done.5) | copy-start | bytes 3145732
  377.5 12.9 %copy-start.1 = (f32[1,96,1536]{2,1,0:T(8,128)S(1)}, f32[1,96,1536]{2,1,0:T(8,128)}, u32[]{:S(2)}) copy-start(f32[1,96,1536]{2,1,0:T(8,128)} %param.11) | copy-start | bytes 1769476
Sparse Core Ops, SparseCore 0:
  81.2 14.7 all-gather.6
  224.8 10.7 all-gather.8
  341.9 9.7 all-gather.10
Sparse Core Ops, SparseCore 1:
  105.2 25.8 reduce-scatter.3
  249.7 21.5 reduce-scatter.5
  367.1 20.5 reduce-scatter.7
